TPU v7x, 32 devices: a 4x4x1 block of a 4x4x4 slice. The times are simulated.
32 devices in a mesh: dp: 2 (over z, core), tp: 16 (over x, y).
Axes of the slice: x: 4, y: 4, z: 1, core: 2. Of those that a mesh axis runs over, the one named last changes fastest.
The devices are a block of a 4x4x4 slice.
Arguments:
- x: bfloat16 [128, 8192], P('dp'), parts along dimension 0
- k_cache: bfloat16 [128, 1024, 64, 128], P('dp', None, 'tp'), parts along dimension 0
- v_cache: bfloat16 [128, 1024, 64, 128], P('dp', None, 'tp'), parts along dimension 0
- gain_a: bfloat16 [8192], replicated
- wq: bfloat16 [8192, 8192], P(None, 'tp')
- wo: bfloat16 [8192, 8192], P('tp')
- gain_m: bfloat16 [8192], replicated
- w_gate: bfloat16 [8192, 24576], P(None, 'tp')
- w_up: bfloat16 [8192, 24576], P(None, 'tp')
- w_down: bfloat16 [24576, 8192], P('tp')
Outputs:
- output: bfloat16 [128, 8192], P('dp'), parts along dimension 0
There are 2 independent parts. A program takes and returns all parts, laid end to end along the dimension named above; an argument that names none is the same for every part.
All inputs are finite; a program needn't handle non-finite values.
Results may differ from a plain program's by a relative error of at most 0.017.
Values are sent between devices in bfloat16 or wider.
A program may use at most 1.5 GiB of HBM per device.

v0:
```python
import jax
import jax.numpy as jnp
from jax import lax
from jax.sharding import PartitionSpec as P

HEAD = 128
THETA = 10000


def normed(x, gain):
    wide = x.astype(jnp.float32)
    scale = lax.rsqrt(jnp.mean(wide * wide, -1, keepdims=True) + 1e-6)
    return (wide * scale * gain.astype(jnp.float32)).astype(jnp.bfloat16)


def turned(t, place, theta):
    half = t.shape[-1] // 2
    angle = place.astype(jnp.float32)[:, None] * theta ** (-jnp.arange(half, dtype=jnp.float32) / half)
    cos, sin = jnp.cos(angle)[:, None], jnp.sin(angle)[:, None]
    a, b = t[..., :half].astype(jnp.float32), t[..., half:].astype(jnp.float32)
    return jnp.concatenate([a * cos - b * sin, b * cos + a * sin], -1).astype(jnp.bfloat16)


def matmul(a, w):
    return jnp.dot(a, w, preferred_element_type=jnp.float32).astype(jnp.bfloat16)


def einsum(form, a, b):
    return jnp.einsum(form, a.astype(jnp.float32), b.astype(jnp.float32))


def seen_by(a, wq, k_cache, v_cache, head, theta):
    batch, cache, kv_heads = k_cache.shape[:3]
    place = jnp.full((batch,), cache - 1)
    q = turned(matmul(a, wq).reshape(batch, -1, head), place, theta).reshape(batch, kv_heads, -1, head)
    scores = einsum("bgsd,bugd->bgsu", q, k_cache) * head**-0.5
    weights = jax.nn.softmax(scores, -1).astype(jnp.bfloat16)
    return einsum("bgsu,bugd->bgsd", weights, v_cache).astype(jnp.bfloat16).reshape(batch, -1)


def hidden_of(b, w_gate, w_up):
    gate = jnp.dot(b, w_gate, preferred_element_type=jnp.float32)
    up = jnp.dot(b, w_up, preferred_element_type=jnp.float32)
    return (jax.nn.silu(gate) * up).astype(jnp.bfloat16)


def solution(mesh):
    def added(t, term):
        return (t.astype(jnp.float32) + lax.psum(term.astype(jnp.bfloat16), "tp").astype(jnp.float32)).astype(jnp.bfloat16)

    def step(x, k_cache, v_cache, gain_a, wq, wo, gain_m, w_gate, w_up, w_down):
        seen = seen_by(normed(x, gain_a), wq, k_cache, v_cache, HEAD, THETA)
        h = added(x, jnp.dot(seen, wo, preferred_element_type=jnp.float32))
        return added(h, jnp.dot(hidden_of(normed(h, gain_m), w_gate, w_up), w_down, preferred_element_type=jnp.float32))

    states, cache, columns, rows_of = P("dp", None), P("dp", None, "tp", None), P(None, "tp"), P("tp", None)
    return jax.shard_map(
        step,
        mesh=mesh,
        in_specs=(states, cache, cache, P(None), columns, rows_of, P(None), columns, columns, rows_of),
        out_specs=states,
        check_vma=False,
    )
```

profile of v0, /device:TPU:96, one launch (start us, length us, event | category | flops | bytes accessed | tf_op | source)
XLA Modules:
  0.0 277.2 jit_solution(6223144677506177114)
XLA Ops:
  6.5 0.0 all-reduce.3.cloned.1.call-start
  6.6 1.5 fusion.7
  8.2 0.7 convert_element_type.66
  8.9 5.3 %convolution_convert_fusion.2 = bf16[64,512]{1,0:T(8,128)(2,1)S(1)} fusion(bf16[8192,512]{1,0:T(8,128)(2,1)} %param.14, bf16[64,8192]{1,0:T(8,128)(2,1)} %param.10, f32[8192]{0:T(1024)S(1)} %convert_element_type.66, f32[64]{0:T(128)S(1)} %add_rsqrt_fusion.1), kind=kOutput, calls=%fused_computation.29 | convolution fusion | flops 539000832 | bytes 9535744 | tf_op jit(solution)/shard_map/dot_general | solution.py:25
  14.3 0.1 fusion.51
  14.4 0.1 maximum_bitcast_fusion
  14.5 30.6 %fusion.4 = f32[64,4,1,1024]{3,2,1,0:T(1,128)S(1)} fusion(bf16[64,1024,4,128]{3,2,1,0:T(4,128)(2,1)} %param.11, bf16[64,4,128,1]{2,0,1,3:T(8,128)(2,1)S(1)} %maximum_bitcast_fusion), kind=kOutput, calls=%fused_computation.4 | convolution fusion | flops 67108864 | bytes 68222976 | tf_op jit(solution)/shard_map/bgsd,bugd->bgsu/dot_general | solution.py:29
  45.1 1.4 fusion.19
  46.6 25.7 %fusion.2 = f32[64,4,1,128]{3,2,1,0:T(1,128)S(1)} fusion(bf16[64,1024,4,128]{3,2,1,0:T(4,128)(2,1)} %param.12, bf16[64,4,1024,1]{2,0,1,3:T(8,128)(2,1)S(1)} %fusion.19), kind=kOutput, calls=%fused_computation.2 | convolution fusion | flops 67108864 | bytes 67764224 | tf_op jit(solution)/shard_map/bgsu,bugd->bgsd/dot_general | solution.py:29
  72.3 0.0 copy-start.1
  72.3 0.0 copy-start
  72.3 6.0 %convolution_convert_fusion.1 = bf16[64,8192]{1,0:T(8,128)(2,1)} fusion(bf16[512,8192]{1,0:T(8,128)(2,1)} %param.15, bf16[8,8,4,128]{3,2,1,0:T(4,128)(2,1)S(1)} %bitcast.22), kind=kOutput, calls=%fused_computation.7 | convolution fusion | flops 537395200 | bytes 9502720 | tf_op jit(solution)/shard_map/dot_general | solution.py:53
  78.3 0.1 all-reduce.3.cloned.1.call-update
  78.4 0.1 all-reduce.5.cloned.1.call-start
  78.5 0.0 copy-done.1
  78.5 79.2 %all-reduce.3.cloned.1.call-done = bf16[64,8192]{1,0:T(8,128)(2,1)} async-done(((bf16[64,8192]{1,0:T(8,128)(2,1)}), bf16[64,8192]{1,0:T(8,128)(2,1)}) %all-reduce.3.cloned.1.call-update) | async-done | bytes 1048592 | tf_op jit(solution)/shard_map/psum | solution.py:49
  157.7 0.0 copy-done
  157.7 1.7 fusion.11
  159.4 10.5 %fusion.33 = f32[64,1536]{1,0:T(8,128)S(1)} fusion(bf16[8192,1536]{1,0:T(8,128)(2,1)} %param.17, bf16[64,8192]{1,0:T(8,128)(2,1)S(1)} %get-tuple-element.6, f32[8192]{0:T(1024)S(1)} %convert_element_type.77, f32[64]{0:T(128)S(1)} %add_rsqrt_fusion), kind=kOutput, calls=%fused_computation.41 | convolution fusion | flops 1612709888 | bytes 26640640 | tf_op jit(solution)/shard_map/dot_general | solution.py:42
  170.0 21.8 %convolution_convert_fusion = bf16[64,8192]{1,0:T(8,128)(2,1)} fusion(bf16[1536,8192]{1,0:T(8,128)(2,1)} %param.19, bf16[8192,1536]{1,0:T(8,128)(2,1)} %param.18, f32[64,1536]{1,0:T(8,128)S(1)} %fusion.33, bf16[64,8192]{1,0:T(8,128)(2,1)S(1)} %get-tuple-element.6, f32[8192]{0:T(1024)S(1)} %convert_element_type.77, f32[64]{0:T(128)S(1)} %add_rsqrt_fusion), kind=kOutput, calls=%fused_computation.6 | convolution fusion | flops 3224436736 | bytes 52855040 | tf_op jit(solution)/shard_map/dot_general | solution.py:54
  191.8 0.1 all-reduce.5.cloned.1.call-update
  191.8 76.1 %all-reduce.5.cloned.1.call-done = bf16[64,8192]{1,0:T(8,128)(2,1)} async-done(((bf16[64,8192]{1,0:T(8,128)(2,1)}), bf16[64,8192]{1,0:T(8,128)(2,1)}) %all-reduce.5.cloned.1.call-update) | async-done | bytes 1048592 | tf_op jit(solution)/shard_map/psum | solution.py:49
  267.9 2.4 fusion.14
  (7 shorter events, 0.2 us)
Async XLA Ops:
  6.5 151.2 %all-reduce.3.cloned.1.call-start = ((), (), s32[]{:S(2)}) async-start(), calls=%async_computation | async-start | bytes 2097152 | tf_op jit(solution)/shard_map/psum | solution.py:49
  72.3 6.2 %copy-start.1 = (bf16[8192]{0:T(1024)(128)(2,1)S(1)}, bf16[8192]{0:T(1024)(128)(2,1)}, u32[]{:S(2)}) copy-start(bf16[8192]{0:T(1024)(128)(2,1)} %param.16) | copy-start | bytes 49156
  72.3 85.4 %copy-start = (bf16[64,8192]{1,0:T(8,128)(2,1)S(1)}, bf16[64,8192]{1,0:T(8,128)(2,1)}, u32[]{:S(2)}) copy-start(bf16[64,8192]{1,0:T(8,128)(2,1)} %param.10) | copy-start | bytes 3145732
  78.4 189.5 %all-reduce.5.cloned.1.call-start = ((), (), s32[]{:S(2)}) async-start(), calls=%async_computation.1 | async-start | bytes 2097152 | tf_op jit(solution)/shard_map/psum | solution.py:49
Sparse Core Ops, SparseCore 0:
  78.5 79.1 all-reduce.2
  192.0 75.8 all-reduce.4
where the time goes:
time: 278 us; the launch traced here: 277 us
  waiting for transfers between devices  155 us (56%)
  matrix products  100 us (36%)
  between operations  13.5 us (5%)
  other arithmetic  8.04 us (3%)
    psum x2, waiting for transfers between devices, added(): lax.psum(term.astype(jnp.bfloat16), 'tp').astype(jnp.float32)  155 us
    dot_general x2, matrix products, einsum(): return jnp.einsum(form, a.astype(jnp.float32), b.astype(jnp.float32))  56.3 us
    dot_general x1, matrix products, step(): jnp.dot(hidden_of(normed(h, gain_m), w_gate, w_up), w_down, preferred_ele...  21.8 us
    dot_general x1, matrix products, hidden_of(): gate = jnp.dot(b, w_gate, preferred_element_type=jnp.float32)  10.5 us
    dot_general x1, matrix products, step(): h = added(x, jnp.dot(seen, wo, preferred_element_type=jnp.float32))  6.01 us
  transfers between devices with their start and end apart: 2, of which 2 were waited for; matrix products, arithmetic and copies ran while one was open for 0% of the time, Pallas kernels for 0%

commit v1 on v0

--- a/solution.py
+++ b/solution.py
@@ -1,10 +1,19 @@
+import functools
+import math
+
 import jax
 import jax.numpy as jnp
 from jax import lax
+from jax.experimental import pallas as pl
+from jax.experimental.pallas import tpu as pltpu
 from jax.sharding import PartitionSpec as P
 
 HEAD = 128
 THETA = 10000
+BF16, F32 = jnp.bfloat16, jnp.float32
+MESH = pl.DeviceIdType.MESH
+SLOTS = 4
+FAR_FIRST = (2, 1, 3)
 
 
 def normed(x, gain):
@@ -38,20 +47,242 @@
     return einsum("bgsu,bugd->bgsd", weights, v_cache).astype(jnp.bfloat16).reshape(batch, -1)
 
 
-def hidden_of(b, w_gate, w_up):
-    gate = jnp.dot(b, w_gate, preferred_element_type=jnp.float32)
-    up = jnp.dot(b, w_up, preferred_element_type=jnp.float32)
-    return (jax.nn.silu(gate) * up).astype(jnp.bfloat16)
+def dot(a, w):
+    return jnp.dot(a, w, preferred_element_type=F32)
+
+
+def tail_kernel(side, seen, x, gain, wo, w_gate, w_up, w_down, out, wg, wu, dn, xp, hp, term, own1, got1, sent2, own2, got2, ag, b, gacc, uacc, hid,
+                x_sem, wo_sem, g_sem, u_sem, d_sem, s1, r1, s2, r2, sv, rv, su, ru):
+    me = lax.axis_index("tp")
+    at = (me // side, me % side)
+    rows, depth = seen.shape
+    d, ff = w_gate.shape
+    wide = d // (2 * side)
+    w = wide // side
+    bk = depth
+    bn = wide // 2
+    nk = d // bk
+    order = FAR_FIRST + (0,)
+    steps = [(g, h) for g in order for h in range(2)]
+
+    def peer(axis, g):
+        place = [at[0], at[1]]
+        place[axis] = lax.rem(at[axis] + g, side)
+        return {"tp": place[0] * side + place[1]}
+
+    def first_column(h, g):
+        return pl.multiple_of((h * side + lax.rem(at[h] + g, side)) * wide, wide)
+
+    across = ff // bn
+    wo_rows = -(-2 * len(steps) // across)
+
+    def wo_piece(j):
+        g, h = steps[j // 2]
+        home = wu.at[pl.ds((nk - wo_rows + j // across) * bk, bk), pl.ds((j % across) * bn, bn)]
+        return pltpu.make_async_copy(wo.at[:, pl.ds(pl.multiple_of(first_column(h, g) + (j % 2) * bn, bn), bn)], home, wo_sem.at[j]), home
+
+    def gate_piece(k):
+        part = pl.ds(pl.multiple_of(k * bk, bk), bk)
+        return pltpu.make_async_copy(w_gate.at[part, :], wg.at[part, :], g_sem.at[k])
+
+    def up_piece(k):
+        part = pl.ds(pl.multiple_of(k * bk, bk), bk)
+        return pltpu.make_async_copy(w_up.at[part, :], wu.at[part, :], u_sem.at[k])
+
+    def down_piece(j):
+        g, h = steps[j // 2]
+        return pltpu.make_async_copy(w_down.at[:, pl.ds(pl.multiple_of(first_column(h, g) + (j % 2) * bn, bn), bn)], dn.at[j % SLOTS], d_sem.at[j % SLOTS])
+
+    def x_piece(h):
+        return pltpu.make_async_copy(x.at[:, pl.ds(pl.multiple_of(first_column(h, 0) + at[1 - h] * w, w), w)], xp.at[h], x_sem.at[h])
+
+    barrier = pltpu.get_barrier_semaphore()
+    for axis in range(2):
+        for g in range(1, side):
+            pl.semaphore_signal(barrier, inc=1, device_id=peer(axis, g), device_id_type=MESH)
+    for j in range(2 * len(steps)):
+        wo_piece(j)[0].start()
+    for h in range(2):
+        x_piece(h).start()
+    for k in range(nk):
+        gate_piece(k).start()
+        if k < nk - wo_rows:
+            up_piece(k).start()
+    for j in range(SLOTS):
+        down_piece(j).start()
+    pl.semaphore_wait(barrier, 2 * (side - 1))
+
+    def summed(piece, base):
+        firsts, seconds, copies = [], [], []
+        for i, (g, h) in enumerate(steps):
+            for c in range(2):
+                value = piece(2 * i + c)
+                if g:
+                    term[h, g - 1, :, pl.ds(c * bn, bn)] = value.astype(BF16)
+                else:
+                    own1[h, :, pl.ds(c * bn, bn)] = value
+            if g:
+                copy = pltpu.make_async_remote_copy(term.at[h, g - 1], got1.at[h, g - 1], s1.at[h, g - 1], r1.at[h, g - 1], device_id=peer(h, g), device_id_type=MESH)
+                copy.start()
+                firsts.append((h, copy))
+        for h in range(2):
+            for half, copy in firsts:
+                if half == h:
+                    copy.wait_recv()
+            for g in order:
+                part = pl.ds(pl.multiple_of(lax.rem(at[1 - h] + g, side) * w, w), w)
+                total = own1[h, :, part]
+                for k in range(side - 1):
+                    total += got1[h, k, :, part].astype(F32)
+                if g:
+                    sent2[h, g - 1] = total.astype(BF16)
+                    copy = pltpu.make_async_remote_copy(sent2.at[h, g - 1], got2.at[h, g - 1], s2.at[h, g - 1], r2.at[h, g - 1], device_id=peer(1 - h, g), device_id_type=MESH)
+                    copy.start()
+                    seconds.append((h, copy))
+                else:
+                    own2[h] = total
+        news, arrivals = {}, []
+        for h in range(2):
+            for half, copy in seconds:
+                if half == h:
+                    copy.wait_recv()
+            total = own2[h]
+            for k in range(side - 1):
+                total += got2[h, k].astype(F32)
+            value = (base(h) + total).astype(BF16)
+            hp[h] = value
+            mine = ag.at[h, at[h], at[1 - h]]
+            mine[...] = value
+            for g in FAR_FIRST:
+                copy = pltpu.make_async_remote_copy(mine, mine, sv.at[h, g - 1], rv.at[h, g - 1], device_id=peer(1 - h, g), device_id_type=MESH)
+                copy.start()
+                news[h, g] = copy
+                copies.append(copy)
+            for g in FAR_FIRST:
+                copy = pltpu.make_async_remote_copy(mine, mine, su.at[h, g - 1, 0], ru.at[h, g - 1, 0], device_id=peer(h, g), device_id_type=MESH)
+                copy.start()
+                copies.append(copy)
+                arrivals.append(copy)
+        for k in (1, 3, 2):
+            for h in range(2):
+                news[h, k].wait_recv()
+                came = ag.at[h, at[h], lax.rem(at[1 - h] + side - k, side)]
+                for g in FAR_FIRST:
+                    copy = pltpu.make_async_remote_copy(came, came, su.at[h, g - 1, k], ru.at[h, g - 1, k], device_id=peer(h, g), device_id_type=MESH)
+                    copy.start()
+                    copies.append(copy)
+                    arrivals.append(copy)
+        for copy in arrivals:
+            copy.wait_recv()
+        for _, copy in firsts + seconds:
+            copy.wait_send()
+        for copy in copies:
+            copy.wait_send()
+
+    def attention_term(j):
+        copy, home = wo_piece(j)
+        copy.wait()
+        value = dot(seen[...], home[...])
+        if j % across == across - 1 or j == 2 * len(steps) - 1:
+            up_piece(nk - wo_rows + j // across).start()
+        return value
+
+    def of_x(h):
+        x_piece(h).wait()
+        return xp[h].astype(F32)
+
+    summed(attention_term, of_x)
+
+    squares = jnp.zeros((rows, w), F32)
+    blocks = [(h, u, v) for h in range(2) for u in range(side) for v in range(side)]
+    for h, u, v in blocks:
+        value = ag[h, u, v].astype(F32)
+        squares += value * value
+    scale = lax.rsqrt(jnp.sum(squares, -1, keepdims=True) / d + 1e-6)
+    for i, (h, u, v) in enumerate(blocks):
+        part = pl.ds(i * w, w)
+        b[:, part] = (ag[h, u, v].astype(F32) * scale * gain[:, part].astype(F32)).astype(BF16)
+
+    gacc[...] = jnp.zeros_like(gacc)
+    uacc[...] = jnp.zeros_like(uacc)
+
+    @pl.loop(0, nk)
+    def _(k):
+        part = pl.ds(pl.multiple_of(k * bk, bk), bk)
+        gate_piece(k).wait()
+        gacc[...] += dot(b[:, part], wg[part, :])
+        up_piece(k).wait()
+        uacc[...] += dot(b[:, part], wu[part, :])
+
+    gate = gacc[...]
+    hid[...] = (gate * jax.nn.sigmoid(gate) * uacc[...]).astype(BF16)
+
+    def mlp_term(j):
+        down_piece(j).wait()
+        value = dot(hid[...], dn[j % SLOTS])
+        if j + SLOTS < 2 * len(steps):
+            down_piece(j + SLOTS).start()
+        return value
+
+    summed(mlp_term, lambda h: hp[h].astype(F32))
+    for i, (h, u, v) in enumerate(blocks):
+        out[:, pl.ds(i * w, w)] = ag[h, u, v]
+
+
+def tail(side, seen, x, gain, wo, w_gate, w_up, w_down):
+    rows, depth = seen.shape
+    d, ff = w_gate.shape
+    wide = d // (2 * side)
+    w = wide // side
+    nk = d // depth
+    hops = side - 1
+    hbm, vmem, dma = pl.BlockSpec(memory_space=pl.ANY), pl.BlockSpec(memory_space=pltpu.VMEM), pltpu.SemaphoreType.DMA
+    return pl.pallas_call(
+        functools.partial(tail_kernel, side),
+        out_shape=jax.ShapeDtypeStruct((rows, d), BF16),
+        in_specs=[vmem, hbm, vmem, hbm, hbm, hbm, hbm],
+        out_specs=vmem,
+        scratch_shapes=[
+            pltpu.VMEM((d, ff), BF16),
+            pltpu.VMEM((d, ff), BF16),
+            pltpu.VMEM((SLOTS, ff, wide // 2), BF16),
+            pltpu.VMEM((2, rows, w), BF16),
+            pltpu.VMEM((2, rows, w), BF16),
+            pltpu.VMEM((2, hops, rows, wide), BF16),
+            pltpu.VMEM((2, rows, wide), F32),
+            pltpu.VMEM((2, hops, rows, wide), BF16),
+            pltpu.VMEM((2, hops, rows, w), BF16),
+            pltpu.VMEM((2, rows, w), F32),
+            pltpu.VMEM((2, hops, rows, w), BF16),
+            pltpu.VMEM((2, side, side, rows, w), BF16),
+            pltpu.VMEM((rows, d), BF16),
+            pltpu.VMEM((rows, ff), F32),
+            pltpu.VMEM((rows, ff), F32),
+            pltpu.VMEM((rows, ff), BF16),
+            dma((2,)),
+            dma((4 * side,)),
+            dma((nk,)),
+            dma((nk,)),
+            dma((SLOTS,)),
+            dma((2, hops)),
+            dma((2, hops)),
+            dma((2, hops)),
+            dma((2, hops)),
+            dma((2, hops)),
+            dma((2, hops)),
+            dma((2, hops, side)),
+            dma((2, hops, side)),
+        ],
+        compiler_params=pltpu.CompilerParams(collective_id=0, has_side_effects=True, vmem_limit_bytes=67043328),
+    )(seen, x, gain.reshape(1, d), wo, w_gate, w_up, w_down)
 
 
 def solution(mesh):
-    def added(t, term):
-        return (t.astype(jnp.float32) + lax.psum(term.astype(jnp.bfloat16), "tp").astype(jnp.float32)).astype(jnp.bfloat16)
+    side = math.isqrt(mesh.shape["tp"])
 
     def step(x, k_cache, v_cache, gain_a, wq, wo, gain_m, w_gate, w_up, w_down):
         seen = seen_by(normed(x, gain_a), wq, k_cache, v_cache, HEAD, THETA)
-        h = added(x, jnp.dot(seen, wo, preferred_element_type=jnp.float32))
-        return added(h, jnp.dot(hidden_of(normed(h, gain_m), w_gate, w_up), w_down, preferred_element_type=jnp.float32))
+        return tail(side, seen, x, gain_m, wo, w_gate, w_up, w_down)
 
     states, cache, columns, rows_of = P("dp", None), P("dp", None, "tp", None), P(None, "tp"), P("tp", None)
     return jax.shard_map(

time: 278 us -> 140 us (0.50)
  waiting for transfers between devices: 155 us -> 0 us
  Pallas kernels: 0 us -> 69.9 us
  matrix products: 100 us -> 61.7 us
  between operations: 13.5 us -> 0.07 us
  local copies, waits for them, and re-layouts: 0.14 us -> 4.37 us
  other arithmetic: 8.04 us -> 3.9 us
    psum x2 -> x0, waiting for transfers between devices: 155 us -> none  [added(): lax.psum(term.astype(jnp.bfloat16), 'tp').astype(jnp.float32)]
    pallas_call x0 -> x1, Pallas kernels: none -> 69.9 us  [tail(): pl.pallas_call(functools.partial(tail_kernel, side), out_shape=jax.ShapeD...]
    dot_general x3 -> x0, matrix products: 38.3 us -> none  [the longest x1 21.8 us: step(): jnp.dot(hidden_of(normed(h, gain_m), w_gate, w_up), w_down, preferred_ele...]
    unnamed x4 -> x2, local copies, waits for them, and re-layouts: 0.01 us -> 2.9 us
  transfers between devices with their start and end apart: 2 -> 0, of which waited for: 2 -> 0; matrix products, arithmetic and copies ran while one was open for 0% -> 0% of each run, Pallas kernels for 0% -> 0%
where the time goes in v1:
time: 140 us
  Pallas kernels  69.9 us (50%)
  matrix products  61.7 us (44%)
  local copies, waits for them, and re-layouts  4.37 us (3%)
  other arithmetic  3.9 us (3%)
    pallas_call x1, Pallas kernels, tail(): pl.pallas_call(functools.partial(tail_kernel, side), out_shape=jax.ShapeD...  69.9 us
    dot_general x2, matrix products, einsum(): return jnp.einsum(form, a.astype(jnp.float32), b.astype(jnp.float32))  56.3 us
    dot_general x1, matrix products, matmul(): jnp.dot(a, w, preferred_element_type=jnp.float32).astype(jnp.bfloat16)  5.35 us
    unnamed x2, local copies, waits for them, and re-layouts  2.9 us

profile of v1, /device:TPU:96, one launch (start us, length us, event | category | flops | bytes accessed | tf_op | source)
XLA Modules:
  0.0 139.9 jit_solution(7369283557712771076)
XLA Ops:
  0.0 1.5 %fusion.6 = f32[64]{0:T(128)S(1)} fusion(bf16[64,8192]{1,0:T(8,128)(2,1)} %x.1), kind=kLoop, calls=%fused_computation.8 | loop fusion | flops 1572800 | bytes 1048832 | tf_op jit(solution)/shard_map/reduce_sum | solution.py:21
  1.5 0.1 fusion.26
  1.6 0.7 convert_element_type.34
  2.3 5.3 %convolution_convert_fusion = bf16[64,512]{1,0:T(8,128)(2,1)S(1)} fusion(bf16[8192,512]{1,0:T(8,128)(2,1)} %param.14, bf16[64,8192]{1,0:T(8,128)(2,1)} %x.1, f32[8192]{0:T(1024)S(1)} %convert_element_type.34, f32[64]{0:T(128)S(1)} %add_rsqrt_fusion), kind=kOutput, calls=%fused_computation.16 | convolution fusion | flops 539000832 | bytes 9535744 | tf_op jit(solution)/shard_map/dot_general | solution.py:34
  7.7 1.3 reshape.57.gain
  9.1 0.1 fusion.31
  9.2 0.1 maximum_bitcast_fusion
  9.3 30.6 %fusion.4 = f32[64,4,1,1024]{3,2,1,0:T(1,128)S(1)} fusion(bf16[64,1024,4,128]{3,2,1,0:T(4,128)(2,1)} %param.11, bf16[64,4,128,1]{2,0,1,3:T(8,128)(2,1)S(1)} %maximum_bitcast_fusion), kind=kOutput, calls=%fused_computation.4 | convolution fusion | flops 67108864 | bytes 68222976 | tf_op jit(solution)/shard_map/bgsd,bugd->bgsu/dot_general | solution.py:38
  39.9 1.4 %fusion.13 = bf16[64,4,1024,1]{2,0,1,3:T(8,128)(2,1)S(1)} fusion(f32[64,4,1,1024]{3,2,1,0:T(1,128)S(1)} %fusion.4), kind=kOutput, calls=%fused_computation.15 | output fusion | flops 1051134 | bytes 1572864 | tf_op jit(solution)/shard_map/div | solution.py:46
  41.4 25.7 %fusion.2 = f32[64,4,1,128]{3,2,1,0:T(1,128)S(1)} fusion(bf16[64,1024,4,128]{3,2,1,0:T(4,128)(2,1)} %param.12, bf16[64,4,1024,1]{2,0,1,3:T(8,128)(2,1)S(1)} %fusion.13), kind=kOutput, calls=%fused_computation.2 | convolution fusion | flops 67108864 | bytes 67764224 | tf_op jit(solution)/shard_map/bgsu,bugd->bgsd/dot_general | solution.py:38
  67.1 0.6 copy.41
  67.7 69.9 %shard_map.100 = bf16[64,8192]{1,0:T(8,128)(2,1)} custom-call(bf16[64,512]{1,0:T(8,128)(2,1)} %bitcast.19, bf16[64,8192]{1,0:T(8,128)(2,1)} %x.1, bf16[1,8192]{1,0:T(2,128)(2,1)} %reshape.57.gain, bf16[512,8192]{1,0:T(8,128)(2,1)} %wo.1, bf16[8192,1536]{1,0:T(8,128)(2,1)} %w_gate.1, bf16[8192,1536]{1,0:T(8,128)(2,1)} %w_up.1, bf16[1536,8192]{1,0:T(8,128)(2,1)} %w_down.1), custom_call_target="tpu_custom_call" | custom-call | tf_op jit(solution)/shard_map/pallas_call | solution.py:240
  137.7 2.3 %copy.43 = bf16[64,8192]{1,0:T(8,128)(2,1)} copy(bf16[64,8192]{1,0:T(8,128)(2,1)} %shard_map.100) | data formatting | bytes 2097152
  (4 shorter events, 0.1 us)

commit v2 on v1

--- a/solution.py
+++ b/solution.py
@@ -3,55 +3,161 @@
 
 import jax
 import jax.numpy as jnp
+import numpy as np
 from jax import lax
 from jax.experimental import pallas as pl
 from jax.experimental.pallas import tpu as pltpu
 from jax.sharding import PartitionSpec as P
 
-HEAD = 128
 THETA = 10000
 BF16, F32 = jnp.bfloat16, jnp.float32
 MESH = pl.DeviceIdType.MESH
 SLOTS = 4
+KV_SLOTS = 12
+GROUP = 4
+FIRST = 2
+JOINT = 4
 FAR_FIRST = (2, 1, 3)
-
-
-def normed(x, gain):
-    wide = x.astype(jnp.float32)
-    scale = lax.rsqrt(jnp.mean(wide * wide, -1, keepdims=True) + 1e-6)
-    return (wide * scale * gain.astype(jnp.float32)).astype(jnp.bfloat16)
-
-
-def turned(t, place, theta):
-    half = t.shape[-1] // 2
-    angle = place.astype(jnp.float32)[:, None] * theta ** (-jnp.arange(half, dtype=jnp.float32) / half)
-    cos, sin = jnp.cos(angle)[:, None], jnp.sin(angle)[:, None]
-    a, b = t[..., :half].astype(jnp.float32), t[..., half:].astype(jnp.float32)
-    return jnp.concatenate([a * cos - b * sin, b * cos + a * sin], -1).astype(jnp.bfloat16)
-
-
-def matmul(a, w):
-    return jnp.dot(a, w, preferred_element_type=jnp.float32).astype(jnp.bfloat16)
-
-
-def einsum(form, a, b):
-    return jnp.einsum(form, a.astype(jnp.float32), b.astype(jnp.float32))
-
-
-def seen_by(a, wq, k_cache, v_cache, head, theta):
-    batch, cache, kv_heads = k_cache.shape[:3]
-    place = jnp.full((batch,), cache - 1)
-    q = turned(matmul(a, wq).reshape(batch, -1, head), place, theta).reshape(batch, kv_heads, -1, head)
-    scores = einsum("bgsd,bugd->bgsu", q, k_cache) * head**-0.5
-    weights = jax.nn.softmax(scores, -1).astype(jnp.bfloat16)
-    return einsum("bgsu,bugd->bgsd", weights, v_cache).astype(jnp.bfloat16).reshape(batch, -1)
 
 
 def dot(a, w):
     return jnp.dot(a, w, preferred_element_type=F32)
 
 
-def tail_kernel(side, seen, x, gain, wo, w_gate, w_up, w_down, out, wg, wu, dn, xp, hp, term, own1, got1, sent2, own2, got2, ag, b, gacc, uacc, hid,
+def head_kernel(heads, x, gain, cos, sin, wq, k, v, seen, xv, a, wqv, kb, vb, gf, qs, os, sc0, sc1, x_sem, w_sem, k_sem, v_sem):
+    rows, d = x.shape
+    head = k.shape[1]
+    span = k.shape[0] // rows
+    slots = kb.shape[0]
+    bk = wqv.shape[0] // w_sem.shape[0]
+    scale = head**-0.5
+    scores = (sc0, sc1)
+
+    def k_piece(s):
+        return pltpu.make_async_copy(k.at[pl.ds(pl.multiple_of(s * span, span), span), :], kb.at[lax.rem(s, slots)], k_sem.at[lax.rem(s, slots)])
+
+    def v_piece(s):
+        return pltpu.make_async_copy(v.at[pl.ds(pl.multiple_of(s * span, span), span), :], vb.at[lax.rem(s, slots)], v_sem.at[lax.rem(s, slots)])
+
+    def w_piece(i):
+        return pltpu.make_async_copy(wq.at[pl.ds(i * bk, bk), :], wqv.at[pl.ds(i * bk, bk), :], w_sem.at[i])
+
+    fetch_x = pltpu.make_async_copy(x, xv, x_sem)
+    fetch_x.start()
+    fetch_x.wait()
+    for i in range(w_sem.shape[0]):
+        w_piece(i).start()
+    for s in range(FIRST):
+        k_piece(s).start()
+        v_piece(s).start()
+    gf[...] = gain[...].astype(F32)
+    qs[...] = jnp.zeros_like(qs)
+    squares = jnp.zeros((rows, 128), F32)
+    for i in range(d // 128):
+        value = xv[:, pl.ds(i * 128, 128)].astype(F32)
+        squares += value * value
+    norm = lax.rsqrt(jnp.sum(squares, -1, keepdims=True) / d + 1e-6)
+    for i in range(d // 128):
+        part = pl.ds(i * 128, 128)
+        a[:, part] = (xv[:, part].astype(F32) * norm * gf[pl.ds(i, 1), :]).astype(BF16)
+    q = jnp.zeros((rows, heads * head), F32)
+    for i in range(w_sem.shape[0]):
+        if i == w_sem.shape[0] // 2:
+            for s in range(FIRST, slots):
+                k_piece(s).start()
+                v_piece(s).start()
+        w_piece(i).wait()
+        q += dot(a[:, pl.ds(i * bk, bk)], wqv[pl.ds(i * bk, bk), :])
+    q = q.astype(BF16).astype(F32)
+    for h in range(heads):
+        one = q[:, h * head : (h + 1) * head]
+        other = jnp.concatenate([one[:, head // 2 :], one[:, : head // 2]], -1)
+        qs[:, h, :] = one * cos[...] + other * sin[...]
+
+    own = lax.rem(lax.broadcasted_iota(jnp.int32, (qs.shape[1], 128), 1), heads) == lax.rem(lax.broadcasted_iota(jnp.int32, (qs.shape[1], 128), 0), heads)
+
+    def score(s, out):
+        out[...] = lax.dot_general(qs[s].astype(BF16), kb[lax.rem(s, slots)], (((1,), (1,)), ((), ())), preferred_element_type=F32)
+
+    def weigh(s, given):
+        pieces = [jnp.where(own, given[:, pl.ds(i * 128, 128)] * scale, -jnp.inf) for i in range(span // 128)]
+        top = functools.reduce(jnp.maximum, pieces)
+        top = jnp.max(top, -1, keepdims=True)
+        pieces = [jnp.exp(p - top) for p in pieces]
+        total = functools.reduce(jnp.add, pieces)
+        share = 1.0 / jnp.sum(total, -1, keepdims=True)
+        weights = jnp.concatenate([(p * share).astype(BF16) for p in pieces], -1)
+        os[s] = dot(weights, vb[lax.rem(s, slots)])
+
+    def refill(piece, s):
+        @pl.when(s + slots < rows)
+        def _():
+            piece(s + slots).start()
+
+    k_piece(0).wait()
+    score(0, scores[0])
+    refill(k_piece, jnp.int32(0))
+
+    def steps(base, count, more):
+        for i in range(count):
+            if i + 1 < count or more:
+                k_piece(base + i + 1).wait()
+            v_piece(base + i).wait()
+        for i in range(count):
+            if i + 1 < count or more:
+                score(base + i + 1, scores[(i + 1) % 2])
+            weigh(base + i, scores[i % 2])
+        for i in range(count):
+            if more:
+                refill(k_piece, base + i + 1)
+                refill(v_piece, base + i)
+
+    @pl.loop(0, rows // GROUP - 1)
+    def _(j):
+        steps(j * GROUP, GROUP, True)
+
+    steps(jnp.int32(rows - GROUP), GROUP, False)
+    for h in range(heads):
+        seen[:, pl.ds(h * head, head)] = os[:, h, :].astype(BF16)
+
+
+def attention(x, k_cache, v_cache, gain, wq):
+    rows, cache, heads, head = k_cache.shape
+    d, out = wq.shape
+    half = head // 2
+    angle = (cache - 1) * float(THETA) ** (-np.arange(half) / half)
+    cos, sin = np.cos(angle), np.sin(angle)
+    turn = [np.concatenate(pair)[None].astype(np.float32) for pair in ((cos, cos), (-sin, sin))]
+    span = cache * heads
+    pad = -(-heads // 8) * 8
+    hbm, vmem, dma = pl.BlockSpec(memory_space=pl.ANY), pl.BlockSpec(memory_space=pltpu.VMEM), pltpu.SemaphoreType.DMA
+    return pl.pallas_call(
+        functools.partial(head_kernel, heads),
+        out_shape=jax.ShapeDtypeStruct((rows, out), BF16),
+        in_specs=[hbm, vmem, vmem, vmem, hbm, hbm, hbm],
+        out_specs=vmem,
+        scratch_shapes=[
+            pltpu.VMEM((rows, d), BF16),
+            pltpu.VMEM((rows, d), BF16),
+            pltpu.VMEM((d, out), BF16),
+            pltpu.VMEM((KV_SLOTS, span, head), BF16),
+            pltpu.VMEM((KV_SLOTS, span, head), BF16),
+            pltpu.VMEM((d // 128, 128), F32),
+            pltpu.VMEM((rows, pad, head), F32),
+            pltpu.VMEM((rows, pad, head), F32),
+            pltpu.VMEM((pad, span), F32),
+            pltpu.VMEM((pad, span), F32),
+            dma,
+            dma((8,)),
+            dma((KV_SLOTS,)),
+            dma((KV_SLOTS,)),
+        ],
+        compiler_params=pltpu.CompilerParams(vmem_limit_bytes=67043328),
+        cost_estimate=pl.CostEstimate(flops=4 * rows * span * head * heads, bytes_accessed=4 * rows * span * head, transcendentals=0),
+    )(x, gain.reshape(d // 128, 128), *turn, wq, k_cache.reshape(rows * span, head), v_cache.reshape(rows * span, head))
+
+
+def tail_kernel(side, seen, x, gain, wo, w_gate, w_up, w_down, out, wg, wu, dn, xp, hp, term, own1, got1, sent2, own2, got2, ag, gf, b, gacc, uacc, hid,
                 x_sem, wo_sem, g_sem, u_sem, d_sem, s1, r1, s2, r2, sv, rv, su, ru):
     me = lax.axis_index("tp")
     at = (me // side, me % side)
@@ -199,19 +305,22 @@
         value = ag[h, u, v].astype(F32)
         squares += value * value
     scale = lax.rsqrt(jnp.sum(squares, -1, keepdims=True) / d + 1e-6)
+    gf[...] = gain[...].astype(F32)
     for i, (h, u, v) in enumerate(blocks):
-        part = pl.ds(i * w, w)
-        b[:, part] = (ag[h, u, v].astype(F32) * scale * gain[:, part].astype(F32)).astype(BF16)
+        for c in range(w // 128):
+            value = ag[h, u, v, :, pl.ds(c * 128, 128)].astype(F32)
+            b[:, pl.ds(i * w + c * 128, 128)] = (value * scale * gf[pl.ds(i * (w // 128) + c, 1), :]).astype(BF16)
 
     gacc[...] = jnp.zeros_like(gacc)
     uacc[...] = jnp.zeros_like(uacc)
 
-    @pl.loop(0, nk)
-    def _(k):
-        part = pl.ds(pl.multiple_of(k * bk, bk), bk)
-        gate_piece(k).wait()
+    @pl.loop(0, nk // JOINT)
+    def _(m):
+        for k in range(JOINT):
+            gate_piece(m * JOINT + k).wait()
+            up_piece(m * JOINT + k).wait()
+        part = pl.ds(pl.multiple_of(m * JOINT * bk, JOINT * bk), JOINT * bk)
         gacc[...] += dot(b[:, part], wg[part, :])
-        up_piece(k).wait()
         uacc[...] += dot(b[:, part], wu[part, :])
 
     gate = gacc[...]
@@ -255,6 +364,7 @@
             pltpu.VMEM((2, rows, w), F32),
             pltpu.VMEM((2, hops, rows, w), BF16),
             pltpu.VMEM((2, side, side, rows, w), BF16),
+            pltpu.VMEM((d // 128, 128), F32),
             pltpu.VMEM((rows, d), BF16),
             pltpu.VMEM((rows, ff), F32),
             pltpu.VMEM((rows, ff), F32),
@@ -274,14 +384,14 @@
             dma((2, hops, side)),
         ],
         compiler_params=pltpu.CompilerParams(collective_id=0, has_side_effects=True, vmem_limit_bytes=67043328),
-    )(seen, x, gain.reshape(1, d), wo, w_gate, w_up, w_down)
+    )(seen, x, gain.reshape(d // 128, 128), wo, w_gate, w_up, w_down)
 
 
 def solution(mesh):
     side = math.isqrt(mesh.shape["tp"])
 
     def step(x, k_cache, v_cache, gain_a, wq, wo, gain_m, w_gate, w_up, w_down):
-        seen = seen_by(normed(x, gain_a), wq, k_cache, v_cache, HEAD, THETA)
+        seen = attention(x, k_cache, v_cache, gain_a, wq)
         return tail(side, seen, x, gain_m, wo, w_gate, w_up, w_down)
 
     states, cache, columns, rows_of = P("dp", None), P("dp", None, "tp", None), P(None, "tp"), P("tp", None)

time: 140 us -> 116 us (0.83)
  matrix products: 61.7 us -> 0 us
  Pallas kernels: 69.9 us -> 113 us
  other arithmetic: 3.9 us -> 0 us
  local copies, waits for them, and re-layouts: 4.37 us -> 2.26 us
    dot_general x3 -> x0, matrix products: 61.7 us -> none  [the longest x2 56.3 us: einsum(): return jnp.einsum(form, a.astype(jnp.float32), b.astype(jnp.float32))]
    pallas_call x0 -> x1, Pallas kernels: none -> 46.7 us  [attention(): pl.pallas_call(functools.partial(head_kernel, heads), out_shape=jax.Shape...]
    pallas_call x1, Pallas kernels: 69.9 us -> 66.7 us  [tail(): pl.pallas_call(functools.partial(tail_kernel, side), out_shape=jax.ShapeD...]
    reduce_sum x1 -> x0, other arithmetic: 1.53 us -> none  [normed(): scale = lax.rsqrt(jnp.mean(wide * wide, -1, keepdims=True) + 1e-06)]
    div x1 -> x0, other arithmetic: 1.42 us -> none  [seen_by(): weights = jax.nn.softmax(scores, -1).astype(jnp.bfloat16)]
    unnamed x2 -> x1, local copies, waits for them, and re-layouts: 2.9 us -> 2.26 us
where the time goes in v2:
time: 116 us
  Pallas kernels  113 us (97%)
  local copies, waits for them, and re-layouts  2.26 us (2%)
    pallas_call x1, Pallas kernels, tail(): pl.pallas_call(functools.partial(tail_kernel, side), out_shape=jax.ShapeD...  66.7 us
    pallas_call x1, Pallas kernels, attention(): pl.pallas_call(functools.partial(head_kernel, heads), out_shape=jax.Shape...  46.7 us

profile of v2, /device:TPU:96, one launch (start us, length us, event | category | flops | bytes accessed | tf_op | source)
XLA Modules:
  0.0 115.7 jit_solution(17027024020485583489)
XLA Ops:
  0.0 46.7 %shard_map.118.seen = bf16[64,512]{1,0:T(8,128)(2,1)} custom-call(bf16[64,8192]{1,0:T(8,128)(2,1)} %x.3, bf16[64,128]{1,0:T(8,128)(2,1)} %bitcast.5, f32[1,128]{1,0:T(1,128)} %constant.4.clone.cos, f32[1,128]{1,0:T(1,128)} %constant.5.clone.sin, bf16[8192,512]{1,0:T(8,128)(2,1)} %wq.1, bf16[262144,128]{1,0:T(8,128)(2,1)} %bitcast.1.k, ...), custom_call_target="tpu_custom_call" | custom-call | flops 536870912 | bytes 134217728 | tf_op jit(solution)/shard_map/pallas_call | solution.py:134
  46.7 66.7 %shard_map.119 = bf16[64,8192]{1,0:T(8,128)(2,1)} custom-call(bf16[64,512]{1,0:T(8,128)(2,1)} %shard_map.118.seen, bf16[64,8192]{1,0:T(8,128)(2,1)} %x.3, bf16[64,128]{1,0:T(8,128)(2,1)} %bitcast.4, bf16[512,8192]{1,0:T(8,128)(2,1)} %wo.1, bf16[8192,1536]{1,0:T(8,128)(2,1)} %w_gate.1, bf16[8192,1536]{1,0:T(8,128)(2,1)} %w_up.1, bf16[1536,8192]{1,0:T(8,128)(2,1)} %w_down.1), custom_call_target="tpu_custom_call" | custom-call | tf_op jit(solution)/shard_map/pallas_call | solution.py:349
  113.4 2.3 %copy.14 = bf16[64,8192]{1,0:T(8,128)(2,1)} copy(bf16[64,8192]{1,0:T(8,128)(2,1)} %shard_map.119) | data formatting | bytes 2097152

commit v3 on v0

v3 whole, which is shorter than its diff:
```python
import functools
import math

import jax
import jax.numpy as jnp
import numpy as np
from jax import lax
from jax.experimental import pallas as pl
from jax.experimental.pallas import tpu as pltpu
from jax.sharding import PartitionSpec as P

THETA = 10000
BF16, F32 = jnp.bfloat16, jnp.float32
MESH = pl.DeviceIdType.MESH
LANES = 128
SLOTS = 4
GROUP = 4
FIRST = 2
JOINT = 8
FAR_FIRST = (2, 1, 3)
SHORT = (False, False, True)
SHORT_LAST = True
CHUNKS = (4, 2, 2)
EVENTS = {8: [(0, 0)], 5: [(0, 1)], 4: [(1, 0)], 3: [(0, 2)], 2: [(1, 1)], 1: [(0, 3)], 0: [(2, 0), (1, 2), (2, 1), (1, 3), (2, 2), (0, 4), (2, 3), (1, 4), (2, 4)]}


def dot(a, w):
    return jnp.dot(a, w, preferred_element_type=F32)


def kernel(side, heads, x, gain_a, gain_m, cos, sin, wq, k, v, wo, w_gate, w_up, w_down, out,
           wg, wu, dn, term, own1, got1, sent2, own2, got2, partial, ag, gf, b, qs, os, sc0, sc1, seen, gacc, uacc, hid,
           x_sem, wq_sem, k_sem, v_sem, wo_sem, g_sem, u_sem, d_sem, s1, r1, s2, r2, sv, rv, su, ru):
    me = lax.axis_index("tp")
    at = (me // side, me % side)
    rows, d = x.shape
    head = k.shape[1]
    span = k.shape[0] // rows
    depth = heads * head
    ff = w_gate.shape[1]
    wide = d // (2 * side)
    w = wide // side
    bk = depth
    bn = wide // 2
    narrow = w // 2
    nk = d // bk
    order = FAR_FIRST + (0,)
    steps = [(g, h) for g in order for h in range(2)]
    pieces_of = [(c, h, u, t) for c in range(2) for h in range(2) for u in range(side) for t in range(side)]

    def peer(axis, g):
        place = [at[0], at[1]]
        place[axis] = lax.rem(at[axis] + g, side)
        return {"tp": place[0] * side + place[1]}

    def group(c, h, g):
        return pl.ds(pl.multiple_of(((c * 2 + h) * side + lax.rem(at[h] + g, side)) * bn, bn), bn)

    strips = (ff - depth) // LANES
    k_slots, v_slots = strips * (d // span), ff // LANES

    def k_home(s):
        i = lax.rem(s, k_slots)
        return pl.ds(pl.multiple_of(i // strips * span, span), span), pl.ds(pl.multiple_of(depth + lax.rem(i, strips) * LANES, LANES), LANES)

    def v_home(s):
        return pl.ds(0, span), pl.ds(pl.multiple_of(lax.rem(s, v_slots) * LANES, LANES), LANES)

    def k_piece(s):
        return pltpu.make_async_copy(k.at[pl.ds(pl.multiple_of(s * span, span), span), :], wg.at[k_home(s)], k_sem.at[lax.rem(s, k_slots)])

    def v_piece(s):
        return pltpu.make_async_copy(v.at[pl.ds(pl.multiple_of(s * span, span), span), :], wu.at[v_home(s)], v_sem.at[lax.rem(s, v_slots)])

    n_wq = wq_sem.shape[0]

    def wq_piece(i):
        part = pl.ds(i * (d // n_wq), d // n_wq)
        return pltpu.make_async_copy(wq.at[part, :], wg.at[part, pl.ds(0, depth)], wq_sem.at[i])

    across = ff // bn
    wo_rows = -(-2 * len(steps) // across)

    def wo_piece(j):
        g, h = steps[j // 2]
        home = wu.at[pl.ds((nk - wo_rows + j // across) * bk, bk), pl.ds((j % across) * bn, bn)]
        return pltpu.make_async_copy(wo.at[:, group(j % 2, h, g)], home, wo_sem.at[j]), home

    def gate_piece(i):
        part = pl.ds(pl.multiple_of(i * bk, bk), bk)
        return pltpu.make_async_copy(w_gate.at[part, :], wg.at[part, :], g_sem.at[i])

    def up_piece(i):
        part = pl.ds(pl.multiple_of(i * bk, bk), bk)
        return pltpu.make_async_copy(w_up.at[part, :], wu.at[part, :], u_sem.at[i])

    def down_piece(j):
        c, (g, h) = j // len(steps), steps[j % len(steps)]
        if j < SLOTS:
            home = dn.at[j]
        else:
            m, i = divmod(j - SLOTS, 2 * across)
            home = (wg, wu)[i // across].at[pl.ds(m * JOINT * bk, ff), pl.ds(i % across * bn, bn)]
        return pltpu.make_async_copy(w_down.at[:, group(c, h, g)], home, d_sem.at[j]), home

    def x_piece(i):
        c, h, u, t = pieces_of[i]
        return pltpu.make_async_copy(x.at[:, pl.ds(i * narrow, narrow)], ag.at[h, u, t, :, pl.ds(c * narrow, narrow)], x_sem.at[i])

    for i in range(len(pieces_of)):
        x_piece(i).start()
    barrier = pltpu.get_barrier_semaphore()
    for axis in range(2):
        for g in range(1, side):
            pl.semaphore_signal(barrier, inc=1, device_id=peer(axis, g), device_id_type=MESH)
    for i in range(n_wq):
        wq_piece(i).start()
    for s in range(FIRST):
        k_piece(jnp.int32(s)).start()
        v_piece(jnp.int32(s)).start()
    qs[...] = jnp.zeros_like(qs)
    for i in range(len(pieces_of)):
        x_piece(i).wait()

    def norm(gain):
        gf[...] = gain[...].astype(F32)
        squares = jnp.zeros((rows, narrow), F32)
        for c, h, u, t in pieces_of:
            value = ag[h, u, t, :, pl.ds(c * narrow, narrow)].astype(F32)
            squares += value * value
        scale = lax.rsqrt(jnp.sum(squares, -1, keepdims=True) / d + 1e-6)
        for i, (c, h, u, t) in enumerate(pieces_of):
            value = ag[h, u, t, :, pl.ds(c * narrow, narrow)].astype(F32)
            b[:, pl.ds(i * narrow, narrow)] = (value * scale * gf[pl.ds(i, 1), :]).astype(BF16)

    norm(gain_a)
    q = jnp.zeros((rows, depth), F32)
    for i in range(n_wq):
        if i == n_wq // 2:
            for s in range(FIRST, k_slots):
                k_piece(jnp.int32(s)).start()
                if s < v_slots:
                    v_piece(jnp.int32(s)).start()
        wq_piece(i).wait()
        part = pl.ds(i * (d // n_wq), d // n_wq)
        q += dot(b[:, part], wg[part, pl.ds(0, depth)])
    q = q.astype(BF16).astype(F32)
    for h in range(heads):
        one = q[:, h * head : (h + 1) * head]
        other = jnp.concatenate([one[:, head // 2 :], one[:, : head // 2]], -1)
        qs[:, h, :] = one * cos[...] + other * sin[...]

    pad = qs.shape[1]
    own = lax.rem(lax.broadcasted_iota(jnp.int32, (pad, LANES), 1), heads) == lax.rem(lax.broadcasted_iota(jnp.int32, (pad, LANES), 0), heads)
    scores = (sc0, sc1)

    def score(s, to):
        to[...] = lax.dot_general(qs[s].astype(BF16), wg[k_home(s)], (((1,), (1,)), ((), ())), preferred_element_type=F32)

    def weigh(s, given):
        pieces = [jnp.where(own, given[:, pl.ds(i * LANES, LANES)] * head**-0.5, -jnp.inf) for i in range(span // LANES)]
        top = jnp.max(functools.reduce(jnp.maximum, pieces), -1, keepdims=True)
        pieces = [jnp.exp(p - top) for p in pieces]
        share = 1.0 / jnp.sum(functools.reduce(jnp.add, pieces), -1, keepdims=True)
        os[s] = dot(jnp.concatenate([(p * share).astype(BF16) for p in pieces], -1), wu[v_home(s)])

    def refill(piece, s):
        @pl.when(s < rows)
        def _():
            piece(s).start()

    def attend(base, more):
        for i in range(GROUP):
            if i + 1 < GROUP or more:
                k_piece(base + i + 1).wait()
            v_piece(base + i).wait()
        for i in range(GROUP):
            if i + 1 < GROUP or more:
                score(base + i + 1, scores[(i + 1) % 2])
            weigh(base + i, scores[i % 2])
        if more:
            for i in range(GROUP):
                refill(k_piece, base + i + 1 + k_slots)
                refill(v_piece, base + i + v_slots)

    class Sum:
        def __init__(self, chunk, r0, nr, cs, ready, piece, short):
            self.chunk, self.part, self.cs, self.ready, self.piece, self.short = chunk, pl.ds(r0, nr), cs, ready, piece, short
            self.group = pl.ds(cs[0] * bn, len(cs) * bn)
            self.block = pl.ds(cs[0] * narrow, len(cs) * narrow)
            self.firsts, self.seconds, self.copies, self.news, self.arrivals = [], [], [], {}, []

        def send(self, source, target, sems, index, device):
            index = (self.chunk,) + index
            copy = pltpu.make_async_remote_copy(source, target, sems[0].at[index], sems[1].at[index], device_id=device, device_id_type=MESH)
            copy.start()
            return copy

        def stage(self, which):
            if self.short:
                (self.terms, self.exchange, self.spread, lambda: None, self.finish)[which]()
            else:
                (self.terms, self.second, self.gather, self.forward, self.finish)[which]()

        def terms(self):
            part, columns = self.part, self.group
            self.ready()
            todo = [(g, h, c) for g, h in steps for c in self.cs]

            def flush(j, value):
                g, h, c = todo[j]
                if not g:
                    own1[h, part, pl.ds(c * bn, bn)] = value
                    return
                term[h, g - 1, part, pl.ds(c * bn, bn)] = value.astype(BF16)
                if c == self.cs[-1]:
                    self.firsts.append((h, self.send(term.at[h, g - 1, part, columns], got1.at[h, g - 1, part, columns], (s1, r1), (h, g - 1), peer(h, g))))

            value = self.piece(0)
            for j in range(1, len(todo)):
                later = self.piece(j)
                flush(j - 1, value)
                value = later
            flush(len(todo) - 1, value)

        def exchange(self):
            part = self.part
            for h in range(2):
                for half, copy in self.firsts:
                    if half == h:
                        copy.wait_recv()
                for c in self.cs:
                    for t in range(side):
                        columns = pl.ds(c * bn + t * narrow, narrow)
                        total = own1[h, part, columns]
                        for i in range(side - 1):
                            total += got1[h, i, part, columns].astype(F32)
                        partial[h, at[1 - h], part, columns] = total.astype(BF16)
                mine = partial.at[h, at[1 - h], part, self.group]
                for g in FAR_FIRST:
                    self.seconds.append((h, self.send(mine, mine, (s2, r2), (h, g - 1), peer(1 - h, g))))

        def spread(self):
            part = self.part
            for h in range(2):
                for half, copy in self.seconds:
                    if half == h:
                        copy.wait_recv()
                for c in self.cs:
                    for t in range(side):
                        columns, narrows = pl.ds(c * bn + t * narrow, narrow), pl.ds(c * narrow, narrow)
                        total = partial[h, 0, part, columns].astype(F32)
                        for i in range(1, side):
                            total += partial[h, i, part, columns].astype(F32)
                        ag[h, at[h], t, part, narrows] = (ag[h, at[h], t, part, narrows].astype(F32) + total).astype(BF16)
                mine = ag.at[h, at[h], :, part, self.block]
                for g in FAR_FIRST:
                    self.arrivals.append(self.send(mine, mine, (su, ru), (h, g - 1, 0), peer(h, g)))

        def second(self):
            part = self.part
            for h in range(2):
                for half, copy in self.firsts:
                    if half == h:
                        copy.wait_recv()
                for g in order:
                    for c in self.cs:
                        columns = pl.ds(pl.multiple_of(c * bn + lax.rem(at[1 - h] + g, side) * narrow, narrow), narrow)
                        total = own1[h, part, columns]
                        for i in range(side - 1):
                            total += got1[h, i, part, columns].astype(F32)
                        if g:
                            sent2[h, g - 1, part, pl.ds(c * narrow, narrow)] = total.astype(BF16)
                        else:
                            own2[h, part, pl.ds(c * narrow, narrow)] = total
                    if g:
                        mine = (h, g - 1, part, self.block)
                        self.seconds.append((h, self.send(sent2.at[mine], got2.at[mine], (s2, r2), (h, g - 1), peer(1 - h, g))))

        def gather(self):
            part, columns = self.part, self.block
            for h in range(2):
                for half, copy in self.seconds:
                    if half == h:
                        copy.wait_recv()
                total = own2[h, part, columns]
                for i in range(side - 1):
                    total += got2[h, i, part, columns].astype(F32)
                mine = ag.at[h, at[h], at[1 - h], part, columns]
                mine[...] = (mine[...].astype(F32) + total).astype(BF16)
                for g in FAR_FIRST:
                    self.news[h, g] = self.send(mine, mine, (sv, rv), (h, g - 1), peer(1 - h, g))
                    self.copies.append(self.news[h, g])
                for g in FAR_FIRST:
                    self.arrivals.append(self.send(mine, mine, (su, ru), (h, g - 1, 0), peer(h, g)))

        def forward(self):
            for i in (1, 3, 2):
                for h in range(2):
                    self.news[h, i].wait_recv()
                    came = ag.at[h, at[h], lax.rem(at[1 - h] + side - i, side), self.part, self.block]
                    for g in FAR_FIRST:
                        self.arrivals.append(self.send(came, came, (su, ru), (h, g - 1, i), peer(h, g)))

        def finish(self):
            for copy in self.arrivals:
                copy.wait_recv()
            for _, copy in self.firsts + self.seconds:
                copy.wait_send()
            for copy in self.copies + self.arrivals:
                copy.wait_send()

    starts = [rows // 8 * sum(CHUNKS[:i]) for i in range(len(CHUNKS))]

    def chunk_sum(c):
        r0, nr = starts[c], rows // 8 * CHUNKS[c]

        def ready():
            if c == 0:
                for j in range(2 * len(steps)):
                    wo_piece(j)[0].wait()

        def piece(j):
            return dot(seen[pl.ds(r0, nr), :], wo_piece(j)[1][...])

        return Sum(c, r0, nr, (0, 1), ready, piece, SHORT[c])

    sums = [chunk_sum(c) for c in range(len(CHUNKS))]

    def run(c, which):
        if which == 0:
            for h in range(heads):
                seen[sums[c].part, pl.ds(h * head, head)] = os[sums[c].part, h, :].astype(BF16)
            if c == 0:
                pl.semaphore_wait(barrier, 2 * (side - 1))
        sums[c].stage(which)
        if which == 0 and c == len(CHUNKS) - 1:
            for i in range(wo_rows):
                up_piece(nk - wo_rows + i).start()

    for j in range(2 * len(steps)):
        wo_piece(j)[0].start()
    k_piece(jnp.int32(0)).wait()
    score(jnp.int32(0), scores[0])
    refill(k_piece, jnp.int32(k_slots))
    groups = rows // GROUP
    early = nk // (d // span)
    begun = groups - k_slots // (d // span) // GROUP - 1
    done = 0
    for back in sorted(set(EVENTS) | {groups - 1 - begun}, reverse=True):
        last = groups - 1 - back
        if back:
            if last + 1 - done > 1:
                @pl.loop(done, last + 1)
                def _(j):
                    attend(j * GROUP, True)
            else:
                attend(jnp.int32(done * GROUP), True)
        else:
            for j in range(done, groups):
                attend(jnp.int32(j * GROUP), j + 1 < groups)
        done = last + 1
        if last == begun:
            for i in range(early):
                gate_piece(i).start()
            for i in range(span // bk, nk - wo_rows):
                up_piece(i).start()
        if not back:
            for i in range(max(nk - early, span // bk)):
                if i < nk - early:
                    gate_piece(early + i).start()
                if i < span // bk:
                    up_piece(i).start()
        for c, which in EVENTS.get(back, ()):
            run(c, which)
            if not back and which == 0:
                for j in range(SLOTS):
                    down_piece(j)[0].start()

    norm(gain_m)
    gacc[...] = jnp.zeros_like(gacc)
    uacc[...] = jnp.zeros_like(uacc)

    @pl.loop(0, nk // JOINT)
    def _(m):
        for i in range(JOINT):
            gate_piece(m * JOINT + i).wait()
            up_piece(m * JOINT + i).wait()
        part = pl.ds(pl.multiple_of(m * JOINT * bk, JOINT * bk), JOINT * bk)
        gacc[...] += dot(b[:, part], wg[part, :])
        uacc[...] += dot(b[:, part], wu[part, :])
        for n in range(-(-(2 * len(steps) - SLOTS) // (2 * across))):

            @pl.when(m == n)
            def _():
                for j in range(SLOTS + n * 2 * across, min(SLOTS + (n + 1) * 2 * across, 2 * len(steps))):
                    down_piece(j)[0].start()

    gate = gacc[...]
    hid[...] = (gate * jax.nn.sigmoid(gate) * uacc[...]).astype(BF16)

    def mlp_sum(c):
        def ready():
            for j in range(len(steps)):
                down_piece(c * len(steps) + j)[0].wait()

        def piece(j):
            return dot(hid[...], down_piece(c * len(steps) + j)[1][...])

        return Sum(c, 0, rows, (c,), ready, piece, SHORT_LAST)

    finals = [mlp_sum(c) for c in range(2)]
    for which in range(5):
        for total in finals:
            total.stage(which)
    for i, (c, h, u, t) in enumerate(pieces_of):
        out[:, pl.ds(i * narrow, narrow)] = ag[h, u, t, :, pl.ds(c * narrow, narrow)]


def layer(side, x, k_cache, v_cache, gain_a, wq, wo, gain_m, w_gate, w_up, w_down):
    rows, cache, heads, head = k_cache.shape
    d, depth = wq.shape
    ff = w_gate.shape[1]
    half = head // 2
    angle = (cache - 1) * float(THETA) ** (-np.arange(half) / half)
    cos, sin = np.cos(angle), np.sin(angle)
    turn = [np.concatenate(pair)[None].astype(np.float32) for pair in ((cos, cos), (-sin, sin))]
    span = cache * heads
    pad = -(-heads // 8) * 8
    wide = d // (2 * side)
    w = wide // side
    nk = d // depth
    hops = side - 1
    chunks = len(CHUNKS)
    hbm, vmem, dma = pl.BlockSpec(memory_space=pl.ANY), pl.BlockSpec(memory_space=pltpu.VMEM), pltpu.SemaphoreType.DMA
    gains = [gain.reshape(d // LANES, LANES) for gain in (gain_a, gain_m)]
    return pl.pallas_call(
        functools.partial(kernel, side, heads),
        out_shape=jax.ShapeDtypeStruct((rows, d), BF16),
        in_specs=[hbm] + [vmem] * 4 + [hbm] * 7,
        out_specs=vmem,
        scratch_shapes=[
            pltpu.VMEM((d, ff), BF16),
            pltpu.VMEM((d, ff), BF16),
            pltpu.VMEM((SLOTS, ff, wide // 2), BF16),
            pltpu.VMEM((2, hops, rows, wide), BF16),
            pltpu.VMEM((2, rows, wide), F32),
            pltpu.VMEM((2, hops, rows, wide), BF16),
            pltpu.VMEM((2, hops, rows, w), BF16),
            pltpu.VMEM((2, rows, w), F32),
            pltpu.VMEM((2, hops, rows, w), BF16),
            pltpu.VMEM((2, side, rows, wide), BF16),
            pltpu.VMEM((2, side, side, rows, w), BF16),
            pltpu.VMEM((d // LANES, LANES), F32),
            pltpu.VMEM((rows, d), BF16),
            pltpu.VMEM((rows, pad, head), F32),
            pltpu.VMEM((rows, pad, head), F32),
            pltpu.VMEM((pad, span), F32),
            pltpu.VMEM((pad, span), F32),
            pltpu.VMEM((rows, depth), BF16),
            pltpu.VMEM((rows, ff), F32),
            pltpu.VMEM((rows, ff), F32),
            pltpu.VMEM((rows, ff), BF16),
            dma((4 * side * side,)),
            dma((8,)),
            dma(((ff - depth) // LANES * (d // span),)),
            dma((ff // LANES,)),
            dma((4 * side,)),
            dma((nk,)),
            dma((nk,)),
            dma((4 * side,)),
            dma((chunks, 2, hops)),
            dma((chunks, 2, hops)),
            dma((chunks, 2, hops)),
            dma((chunks, 2, hops)),
            dma((chunks, 2, hops)),
            dma((chunks, 2, hops)),
            dma((chunks, 2, hops, side)),
            dma((chunks, 2, hops, side)),
        ],
        compiler_params=pltpu.CompilerParams(collective_id=0, has_side_effects=True, vmem_limit_bytes=67043328),
    )(x, *gains, *turn, wq, k_cache.reshape(rows * span, head), v_cache.reshape(rows * span, head), wo, w_gate, w_up, w_down)


def solution(mesh):
    side = math.isqrt(mesh.shape["tp"])
    states, cache, columns, rows_of = P("dp", None), P("dp", None, "tp", None), P(None, "tp"), P("tp", None)
    return jax.shard_map(
        functools.partial(layer, side),
        mesh=mesh,
        in_specs=(states, cache, cache, P(None), columns, rows_of, P(None), columns, columns, rows_of),
        out_specs=states,
        check_vma=False,
    )
```

time: 278 us -> 105 us (0.38)
  waiting for transfers between devices: 155 us -> 0 us
  Pallas kernels: 0 us -> 102 us
  matrix products: 100 us -> 0 us
  between operations: 13.5 us -> 0.01 us
  other arithmetic: 8.04 us -> 0 us
    psum x2 -> x0, waiting for transfers between devices: 155 us -> none  [added(): lax.psum(term.astype(jnp.bfloat16), 'tp').astype(jnp.float32)]
    pallas_call x0 -> x1, Pallas kernels: none -> 102 us  [layer(): pl.pallas_call(functools.partial(kernel, side, heads), out_shape=jax.Shap...]
    dot_general x6 -> x0, matrix products: 100 us -> none  [the longest x2 56.3 us: einsum(): return jnp.einsum(form, a.astype(jnp.float32), b.astype(jnp.float32))]
    reduce_sum x2 -> x0, other arithmetic: 3.23 us -> none  [normed(): scale = lax.rsqrt(jnp.mean(wide * wide, -1, keepdims=True) + 1e-06)]
    convert_element_type x4 -> x0, other arithmetic: 3.19 us -> none  [the longest x1 2.43 us: added(): (t.astype(jnp.float32) + lax.psum(term.astype(jnp.bfloat16), 'tp').astype...]
  transfers between devices with their start and end apart: 2 -> 0, of which waited for: 2 -> 0; matrix products, arithmetic and copies ran while one was open for 0% -> 0% of each run, Pallas kernels for 0% -> 0%
where the time goes in v3:
time: 105 us
  Pallas kernels  102 us (97%)
  local copies, waits for them, and re-layouts  2.26 us (2%)
    pallas_call x1, Pallas kernels, layer(): pl.pallas_call(functools.partial(kernel, side, heads), out_shape=jax.Shap...  102 us
    unnamed x1, local copies, waits for them, and re-layouts  2.26 us

profile of v3, /device:TPU:96, one launch (start us, length us, event | category | flops | bytes accessed | tf_op | source)
XLA Modules:
  0.0 104.5 jit_solution(17504262084402344693)
XLA Ops:
  0.0 102.3 %shard_map.118 = bf16[64,8192]{1,0:T(8,128)(2,1)} custom-call(bf16[64,8192]{1,0:T(8,128)(2,1)} %x.1, bf16[64,128]{1,0:T(8,128)(2,1)} %bitcast.4, bf16[64,128]{1,0:T(8,128)(2,1)} %bitcast.5, f32[1,128]{1,0:T(1,128)} %constant.4.clone.cos, f32[1,128]{1,0:T(1,128)} %constant.5.clone.sin, bf16[8192,512]{1,0:T(8,128)(2,1)} %wq.1, bf16[262144,128]{1,0:T(8,128)(2,1)} %bitcast.2.k, ...), custom_call_target="tpu_custom_call" | custom-call | tf_op jit(solution)/shard_map/pallas_call | solution.py:437
  102.3 2.3 %copy.14 = bf16[64,8192]{1,0:T(8,128)(2,1)} copy(bf16[64,8192]{1,0:T(8,128)(2,1)} %shard_map.118) | data formatting | bytes 2097152

commit v4 on v3

--- a/solution.py
+++ b/solution.py
@@ -16,12 +16,10 @@
 SLOTS = 4
 GROUP = 4
 FIRST = 2
-JOINT = 8
+JOINT = 4
 FAR_FIRST = (2, 1, 3)
-SHORT = (False, False, True)
-SHORT_LAST = True
 CHUNKS = (4, 2, 2)
-EVENTS = {8: [(0, 0)], 5: [(0, 1)], 4: [(1, 0)], 3: [(0, 2)], 2: [(1, 1)], 1: [(0, 3)], 0: [(2, 0), (1, 2), (2, 1), (1, 3), (2, 2), (0, 4), (2, 3), (1, 4), (2, 4)]}
+EVENTS = {8: [(0, 0)], 5: [(0, 1)], 4: [(1, 0)], 3: [(0, 2)], 2: [(1, 1)], 0: [(2, 0), (2, 1), (1, 2), (2, 2), (0, 3), (1, 3), (2, 3)]}
 
 
 def dot(a, w):
@@ -29,8 +27,8 @@
 
 
 def kernel(side, heads, x, gain_a, gain_m, cos, sin, wq, k, v, wo, w_gate, w_up, w_down, out,
-           wg, wu, dn, term, own1, got1, sent2, own2, got2, partial, ag, gf, b, qs, os, sc0, sc1, seen, gacc, uacc, hid,
-           x_sem, wq_sem, k_sem, v_sem, wo_sem, g_sem, u_sem, d_sem, s1, r1, s2, r2, sv, rv, su, ru):
+           wg, wu, dn, term, own1, got1, partial, ag, gf, b, qs, os, sc0, sc1, seen, gacc, uacc, hid,
+           x_sem, wq_sem, k_sem, v_sem, wo_sem, g_sem, u_sem, d_sem, s1, r1, s2, r2, s3, r3):
     me = lax.axis_index("tp")
     at = (me // side, me % side)
     rows, d = x.shape
@@ -44,8 +42,7 @@
     bn = wide // 2
     narrow = w // 2
     nk = d // bk
-    order = FAR_FIRST + (0,)
-    steps = [(g, h) for g in order for h in range(2)]
+    steps = [(g, h) for g in FAR_FIRST + (0,) for h in range(2)]
     pieces_of = [(c, h, u, t) for c in range(2) for h in range(2) for u in range(side) for t in range(side)]
 
     def peer(axis, g):
@@ -184,11 +181,11 @@
                 refill(v_piece, base + i + v_slots)
 
     class Sum:
-        def __init__(self, chunk, r0, nr, cs, ready, piece, short):
-            self.chunk, self.part, self.cs, self.ready, self.piece, self.short = chunk, pl.ds(r0, nr), cs, ready, piece, short
+        def __init__(self, chunk, r0, nr, cs, ready, piece):
+            self.chunk, self.part, self.cs, self.ready, self.piece = chunk, pl.ds(r0, nr), cs, ready, piece
             self.group = pl.ds(cs[0] * bn, len(cs) * bn)
             self.block = pl.ds(cs[0] * narrow, len(cs) * narrow)
-            self.firsts, self.seconds, self.copies, self.news, self.arrivals = [], [], [], {}, []
+            self.firsts, self.seconds, self.arrivals = [], [], []
 
         def send(self, source, target, sems, index, device):
             index = (self.chunk,) + index
@@ -197,10 +194,7 @@
             return copy
 
         def stage(self, which):
-            if self.short:
-                (self.terms, self.exchange, self.spread, lambda: None, self.finish)[which]()
-            else:
-                (self.terms, self.second, self.gather, self.forward, self.finish)[which]()
+            (self.terms, self.exchange, self.spread, self.finish)[which]()
 
         def terms(self):
             part, columns = self.part, self.group
@@ -255,59 +249,14 @@
                         ag[h, at[h], t, part, narrows] = (ag[h, at[h], t, part, narrows].astype(F32) + total).astype(BF16)
                 mine = ag.at[h, at[h], :, part, self.block]
                 for g in FAR_FIRST:
-                    self.arrivals.append(self.send(mine, mine, (su, ru), (h, g - 1, 0), peer(h, g)))
-
-        def second(self):
-            part = self.part
-            for h in range(2):
-                for half, copy in self.firsts:
-                    if half == h:
-                        copy.wait_recv()
-                for g in order:
-                    for c in self.cs:
-                        columns = pl.ds(pl.multiple_of(c * bn + lax.rem(at[1 - h] + g, side) * narrow, narrow), narrow)
-                        total = own1[h, part, columns]
-                        for i in range(side - 1):
-                            total += got1[h, i, part, columns].astype(F32)
-                        if g:
-                            sent2[h, g - 1, part, pl.ds(c * narrow, narrow)] = total.astype(BF16)
-                        else:
-                            own2[h, part, pl.ds(c * narrow, narrow)] = total
-                    if g:
-                        mine = (h, g - 1, part, self.block)
-                        self.seconds.append((h, self.send(sent2.at[mine], got2.at[mine], (s2, r2), (h, g - 1), peer(1 - h, g))))
-
-        def gather(self):
-            part, columns = self.part, self.block
-            for h in range(2):
-                for half, copy in self.seconds:
-                    if half == h:
-                        copy.wait_recv()
-                total = own2[h, part, columns]
-                for i in range(side - 1):
-                    total += got2[h, i, part, columns].astype(F32)
-                mine = ag.at[h, at[h], at[1 - h], part, columns]
-                mine[...] = (mine[...].astype(F32) + total).astype(BF16)
-                for g in FAR_FIRST:
-                    self.news[h, g] = self.send(mine, mine, (sv, rv), (h, g - 1), peer(1 - h, g))
-                    self.copies.append(self.news[h, g])
-                for g in FAR_FIRST:
-                    self.arrivals.append(self.send(mine, mine, (su, ru), (h, g - 1, 0), peer(h, g)))
-
-        def forward(self):
-            for i in (1, 3, 2):
-                for h in range(2):
-                    self.news[h, i].wait_recv()
-                    came = ag.at[h, at[h], lax.rem(at[1 - h] + side - i, side), self.part, self.block]
-                    for g in FAR_FIRST:
-                        self.arrivals.append(self.send(came, came, (su, ru), (h, g - 1, i), peer(h, g)))
+                    self.arrivals.append(self.send(mine, mine, (s3, r3), (h, g - 1), peer(h, g)))
 
         def finish(self):
             for copy in self.arrivals:
                 copy.wait_recv()
             for _, copy in self.firsts + self.seconds:
                 copy.wait_send()
-            for copy in self.copies + self.arrivals:
+            for copy in self.arrivals:
                 copy.wait_send()
 
     starts = [rows // 8 * sum(CHUNKS[:i]) for i in range(len(CHUNKS))]
@@ -323,7 +272,7 @@
         def piece(j):
             return dot(seen[pl.ds(r0, nr), :], wo_piece(j)[1][...])
 
-        return Sum(c, r0, nr, (0, 1), ready, piece, SHORT[c])
+        return Sum(c, r0, nr, (0, 1), ready, piece)
 
     sums = [chunk_sum(c) for c in range(len(CHUNKS))]
 
@@ -407,10 +356,10 @@
         def piece(j):
             return dot(hid[...], down_piece(c * len(steps) + j)[1][...])
 
-        return Sum(c, 0, rows, (c,), ready, piece, SHORT_LAST)
+        return Sum(c, 0, rows, (c,), ready, piece)
 
     finals = [mlp_sum(c) for c in range(2)]
-    for which in range(5):
+    for which in range(4):
         for total in finals:
             total.stage(which)
     for i, (c, h, u, t) in enumerate(pieces_of):
@@ -446,9 +395,6 @@
             pltpu.VMEM((2, hops, rows, wide), BF16),
             pltpu.VMEM((2, rows, wide), F32),
             pltpu.VMEM((2, hops, rows, wide), BF16),
-            pltpu.VMEM((2, hops, rows, w), BF16),
-            pltpu.VMEM((2, rows, w), F32),
-            pltpu.VMEM((2, hops, rows, w), BF16),
             pltpu.VMEM((2, side, rows, wide), BF16),
             pltpu.VMEM((2, side, side, rows, w), BF16),
             pltpu.VMEM((d // LANES, LANES), F32),
@@ -475,8 +421,6 @@
             dma((chunks, 2, hops)),
             dma((chunks, 2, hops)),
             dma((chunks, 2, hops)),
-            dma((chunks, 2, hops, side)),
-            dma((chunks, 2, hops, side)),
         ],
         compiler_params=pltpu.CompilerParams(collective_id=0, has_side_effects=True, vmem_limit_bytes=67043328),
     )(x, *gains, *turn, wq, k_cache.reshape(rows * span, head), v_cache.reshape(rows * span, head), wo, w_gate, w_up, w_down)

time: 105 us -> 103 us (0.981)
    pallas_call x1, Pallas kernels: 102 us -> 101 us  [layer(): pl.pallas_call(functools.partial(kernel, side, heads), out_shape=jax.Shap...]
where the time goes in v4:
time: 103 us
  Pallas kernels  101 us (98%)
  local copies, waits for them, and re-layouts  2.26 us (2%)
    pallas_call x1, Pallas kernels, layer(): pl.pallas_call(functools.partial(kernel, side, heads), out_shape=jax.Shap...  101 us
    unnamed x1, local copies, waits for them, and re-layouts  2.26 us

profile of v4, /device:TPU:96, one launch (start us, length us, event | category | flops | bytes accessed | tf_op | source)
XLA Modules:
  0.0 103.0 jit_solution(15402506721525528925)
XLA Ops:
  0.0 100.8 %shard_map.118 = bf16[64,8192]{1,0:T(8,128)(2,1)} custom-call(bf16[64,8192]{1,0:T(8,128)(2,1)} %x.1, bf16[64,128]{1,0:T(8,128)(2,1)} %bitcast.4, bf16[64,128]{1,0:T(8,128)(2,1)} %bitcast.5, f32[1,128]{1,0:T(1,128)} %constant.4.clone.cos, f32[1,128]{1,0:T(1,128)} %constant.5.clone.sin, bf16[8192,512]{1,0:T(8,128)(2,1)} %wq.1, bf16[262144,128]{1,0:T(8,128)(2,1)} %bitcast.2.k, ...), custom_call_target="tpu_custom_call" | custom-call | tf_op jit(solution)/shard_map/pallas_call | solution.py:386
  100.8 2.3 %copy.14 = bf16[64,8192]{1,0:T(8,128)(2,1)} copy(bf16[64,8192]{1,0:T(8,128)(2,1)} %shard_map.118) | data formatting | bytes 2097152
